TPU v7x, 256 devices: a whole 4x4x8 slice. The times are simulated.
256 devices in a mesh: sims: 4 (over z_hi, core), blk: 64 (over x, z_lo, y).
Axes of the slice: x: 4, y: 4, z: 8 (z_hi: 2, z_lo: 4; z = z_hi * 4 + z_lo), core: 2. Of those that a mesh axis runs over, the one named last changes fastest.
Arguments:
- sim_alm: bfloat16 [1536, 16, 2, 1536], P('blk', 'sims'), may hold values from -6 to 6
- t_filter: float32 [1536], replicated, may hold values from 0.0006510417 to 0.00390625
- wiener_filter: float32 [1536], replicated, may hold values from 8.477105e-07 to 5.086263e-06
- colatitude: float32 [128], replicated, may hold values from 1.09712 to 1.60288, as said below
- legendre: bfloat16 [1536, 1536, 128], P('blk'), may hold values from -2 to 2, as said below
- pixel_mask: int32 [128, 4096], P('blk'), may hold values 0 or 1
Outputs:
- field_sum: float32 [1536, 2, 1536], P('blk', None, 'sims')
- spectra: float32 [16, 2, 1536], P('sims')
Inputs may be any that keep to these rules, and one draw needn't show every extreme that they name: `colatitude`: the colatitudes of 128 cycles in increasing order, about 0.0016 apart, in a band centred between 1.2 and 1.5. legendre[m,l,r] is the orthonormal associated Legendre function of degree l and order m at colatitude[r], zero for l < m, rounded to bfloat16.
All inputs are finite; a program needn't handle non-finite values. No bound on the sum of `pixel_mask` on one device may be relied on, other than what follows from the above.
Results may differ from a plain program's by a relative error of at most 0.006.
The roundings to bfloat16 on the way count: a program that leaves them out, or rounds other values in their place, can miss the bound.
Values may be sent and summed in bfloat16 or wider, within the bound.
No kernel may reach another device: no remote copies, remote signals or barrier semaphores. Data moves between devices by JAX's collectives and lax.ppermute only.
A program may use at most 192 MiB of HBM per device.

v0:
```python
import math
import jax
import jax.numpy as jnp
from jax import lax
from jax.sharding import Mesh
from jax.sharding import PartitionSpec as P

BLK = ("blk_0", "blk_1", "blk_2")


def in_blocks(shard, dim, length):
    before, after = (shard.shape[:dim], shard.shape[dim + 1 :])
    return jnp.moveaxis(shard.reshape(*before, length, -1, *after), dim, 0)


def in_order(pieces, dim):
    pieces = jnp.moveaxis(pieces, 0, dim)
    dims = pieces.shape
    return pieces.reshape(*dims[:dim], dims[dim] * dims[dim + 1], *dims[dim + 2 :])


def exchange_in_order(pieces, axes, turns):
    inside = pieces.shape[1:]
    result = pieces.reshape(*(lax.axis_size(a) for a in axes), *inside)
    for k in turns:
        result = lax.all_to_all(result, axes[k], k, k, tiled=True)
    return result.reshape(-1, *inside)


def exchange_by_axis(shard, axes, turns, split_dim, concat_dim):
    pieces = in_blocks(shard, split_dim, lax.axis_size(axes))
    return in_order(exchange_in_order(pieces, axes, turns), concat_dim)


def from_everyone(shard, axis):
    length = lax.axis_size(axis)
    return lax.all_to_all(
        jnp.broadcast_to(shard[None], (length, *shard.shape)), axis, 0, 0, tiled=True
    )


def taken_together(shard, axis):
    everything = from_everyone(shard, axis)
    return jnp.sum(everything.astype(jnp.float32), axis=0)


def ladder(degree, orders):
    numerator = (2.0 * degree + 1.0) * (degree * degree - orders * orders)
    denominator = jnp.maximum(2.0 * degree - 1.0, 1.0)
    return jnp.where(degree > orders, jnp.sqrt(jnp.maximum(numerator, 0.0) / denominator), 0.0)


def fourier_table(mode_count, pixels):
    mode_ids = jnp.arange(mode_count, dtype=jnp.int32)[:, None]
    pixel_ids = jnp.arange(pixels, dtype=jnp.int32)[None, :]
    phases = 2.0 * math.pi / pixels * (mode_ids * pixel_ids % pixels).astype(jnp.float32)
    return jnp.stack(
        [jnp.cos(phases).astype(jnp.bfloat16), (-jnp.sin(phases)).astype(jnp.bfloat16)], axis=1
    )


def per_device(sim_alm, t_filter, wiener_filter, colatitude, legendre, pixel_mask):
    local_modes = sim_alm.shape[0]
    sims_here = sim_alm.shape[1]
    degrees = sim_alm.shape[3]
    cycle_count = legendre.shape[2]
    pixels = pixel_mask.shape[1]
    blocks = lax.axis_size(BLK)
    cycle_local = cycle_count // blocks
    first_mode = lax.axis_index(BLK) * local_modes
    degree = jnp.arange(degrees, dtype=jnp.float32)
    local_orders = (first_mode + jnp.arange(local_modes, dtype=jnp.int32)).astype(jnp.float32)
    all_orders = jnp.arange(degrees, dtype=jnp.float32)
    ladder_steps = ladder(degree[None, :], local_orders[:, None])
    cotangent = jnp.cos(colatitude) / jnp.sin(colatitude)
    cosecant = 1.0 / jnp.sin(colatitude)
    tilt_grid = jnp.cos(colatitude).reshape(blocks, 1, cycle_local)
    values = sim_alm.astype(jnp.float32)
    weighted = wiener_filter * values
    raised = ladder_steps[:, None, None, :] * weighted
    lowered = jnp.concatenate([raised[..., 1:], jnp.zeros_like(raised[..., :1])], axis=-1)
    coefs = jnp.stack([t_filter * values, weighted, degree * weighted, lowered], axis=1).astype(
        jnp.bfloat16
    )
    flattened = coefs.reshape(local_modes, 8 * sims_here, degrees)
    legsum = jnp.einsum("mkl,mlr->krm", flattened, legendre, preferred_element_type=jnp.float32)
    legsum = legsum.reshape(4, sims_here, 2, cycle_count, local_modes)
    rotated = jnp.stack([-legsum[1][:, 1], legsum[1][:, 0]], axis=1) * (
        cosecant[:, None] * local_orders[None, :]
    )
    slopes = cotangent[:, None] * legsum[2] - cosecant[:, None] * legsum[3]
    cycle_coefs = jnp.stack([legsum[0], rotated, slopes], axis=0).astype(jnp.bfloat16)
    cycle_coefs = cycle_coefs.reshape(3, sims_here, 2, cycle_count * local_modes)
    fourier = fourier_table(degrees, pixels)
    fourier_grid = fourier.reshape(blocks, local_modes, 2, pixels)
    mode_weight = (
        jnp.where(all_orders > 0, 2.0, 1.0).astype(jnp.bfloat16).reshape(blocks, 1, local_modes)
    )
    pixel_weight = pixel_mask.astype(jnp.float32)
    legendre_grid = legendre.reshape(local_modes, degrees, blocks, cycle_local)
    arranged = lax.all_to_all(cycle_coefs, BLK, split_axis=3, concat_axis=3, tiled=True).reshape(
        3, -1, 2, blocks, cycle_local, local_modes
    )
    scaled = arranged * mode_weight
    cycle_maps = jnp.einsum(
        "qscbrn,bncj->qsrj", scaled, fourier_grid, preferred_element_type=jnp.float32
    )
    product = pixel_weight * cycle_maps[0]
    flow_maps = jnp.stack([product * cycle_maps[2], product * cycle_maps[1]]).astype(jnp.bfloat16)
    mode_coefs = jnp.einsum(
        "psrj,mcj->pscmr", flow_maps, fourier, preferred_element_type=jnp.float32
    )
    mode_coefs = (mode_coefs * (2.0 * math.pi / pixels)).astype(jnp.bfloat16)
    mode_coefs = mode_coefs.reshape(2, mode_coefs.shape[1], 2, degrees * cycle_local)
    returned = exchange_by_axis(mode_coefs, BLK, (0, 1, 2), 3, 3)
    returned = returned.reshape(2, -1, 2, blocks, local_modes, cycle_local)
    tilted = (tilt_grid * returned[0].astype(jnp.float32)).astype(jnp.bfloat16)
    stacked = jnp.stack([tilted, returned[0], returned[1]], axis=0)
    projected = jnp.einsum(
        "kscbnr,nlbr->knscl", stacked, legendre_grid, preferred_element_type=jnp.float32
    )
    shifted = jnp.concatenate(
        [jnp.zeros_like(projected[1][..., :1]), projected[1][..., :-1]], axis=-1
    )
    first_part = projected[0]
    third_part = projected[2]
    order_column = local_orders[:, None, None]
    step_rows = ladder_steps[:, None, :]
    real_part = (
        degree * first_part[:, :, 0]
        - step_rows * shifted[:, :, 0]
        + order_column * third_part[:, :, 1]
    )
    imag_part = (
        degree * first_part[:, :, 1]
        - step_rows * shifted[:, :, 1]
        - order_column * third_part[:, :, 0]
    )
    estimates = jnp.stack([real_part, imag_part], axis=2) / degrees
    partial_value = jnp.sum(estimates, axis=1)
    quarter = degrees // lax.axis_size("sims")
    field_total = taken_together(partial_value.astype(jnp.bfloat16), "sims").astype(jnp.float32)
    field_share = lax.dynamic_slice_in_dim(
        field_total, lax.axis_index("sims") * quarter, quarter, 2
    )
    sim_total = sims_here * lax.axis_size("sims")
    residual = estimates - field_total[:, None] / sim_total
    partner = residual.reshape(local_modes, sims_here // 2, 2, 2, degrees)[:, :, ::-1].reshape(
        residual.shape
    )
    auto_power = jnp.sum(residual * residual, axis=2)
    cross_power = jnp.sum(residual * partner, axis=2)
    local_weight = jnp.where(local_orders > 0, 2.0, 1.0)
    local_power = jnp.stack(
        [
            jnp.einsum("m,msl->sl", local_weight, auto_power),
            jnp.einsum("m,msl->sl", local_weight, cross_power),
        ],
        axis=1,
    )
    summed = taken_together(local_power.astype(jnp.bfloat16), BLK).astype(jnp.float32)
    spectra = summed / (2.0 * degree + 1.0)
    return (field_share, spectra)


def solution(mesh):
    torus = Mesh(
        mesh.devices.reshape(mesh.shape["sims"], 4, 4, 4), ("sims", "blk_0", "blk_1", "blk_2")
    )
    return jax.shard_map(
        per_device,
        mesh=torus,
        in_specs=(P(BLK, "sims", None, None), P(), P(), P(), P(BLK, None, None), P(BLK, None)),
        out_specs=(P(BLK, None, "sims"), P("sims", None, None)),
        check_vma=False,
    )
```

profile of v0, /device:TPU:1, one launch (start us, length us, event | category | flops | bytes accessed | tf_op | source)
XLA Modules:
  0.0 460.9 jit_solution(1568018498141478940)
XLA Ops:
  0.9 0.5 copy-done
  1.4 2.4 convert_bitcast_fusion
  3.8 1.3 fusion.24
  5.1 0.5 pad_bitcast_fusion
  5.6 4.6 pad_maximum_fusion
  10.2 3.9 copy.204
  14.0 5.0 %convert_element_type.158 = bf16[24,32,1536]{2,1,0:T(8,128)(2,1)S(1)} reshape(bf16[24,4,4,2,1536]{4,3,2,1,0:T(2,128)(2,1)} %copy.204) | data formatting | bytes 4718592 | tf_op jit(solution)/shard_map/convert_element_type | solution.py:82
  19.0 4.6 %convolution_bitcast_fusion = f32[32,128,24]{1,0,2:T(8,128)S(1)} fusion(bf16[24,32,1536]{2,1,0:T(8,128)(2,1)S(1)} %convert_element_type.158, bf16[24,1536,128]{2,1,0:T(8,128)(2,1)} %param.10), kind=kOutput, calls=%fused_computation.37 | convolution fusion | flops 301989888 | bytes 12189696 | tf_op jit(solution)/shard_map/mkl,mlr->krm/dot_general | solution.py:86
  24.0 0.2 stack.93
  24.3 0.2 stack.94
  24.7 0.5 copy-done.5
  25.4 0.2 copy.210
  25.6 0.3 squeeze.15
  26.0 0.2 copy.211
  26.2 0.3 squeeze.16
  26.9 0.3 stack.78
  27.4 0.2 pad_maximum_fusion.1
  27.7 8.1 %copy.212 = bf16[3,4,2,3072]{1,2,0,3:T(2,128)(2,1)} copy(bf16[3,4,2,3072]{3,2,1,0:T(2,128)(2,1)S(1)} %pad_maximum_fusion.1) | data formatting | bytes 294912 | tf_op jit(solution)/shard_map/stack | solution.py:92
  35.7 12.9 %reshape.533 = bf16[64,2,576]{2,1,0:T(2,128)(2,1)} reshape(bf16[3072,3,2,4]{3,2,1,0:T(2,128)(2,1)} %bitcast.120) | data formatting | bytes 294912
  48.6 12.5 %all-to-all-start = ((bf16[64,2,576]{2,1,0:T(2,128)(2,1)}), bf16[64,2,576]{2,1,0:T(2,128)(2,1)S(1)}, u32[]{:S(2)}, u32[]{:S(2)}) async-start(bf16[64,2,576]{2,1,0:T(2,128)(2,1)} %reshape.533), calls=%async_computation | async-start | bytes 327680 | tf_op jit(solution)/shard_map/all_to_all | solution.py:101
  61.1 101.2 %negate_convert_fusion.1 = (bf16[1536,1,4096]{2,0,1:T(8,128)(2,1)}, bf16[1536,1,4096]{2,0,1:T(8,128)(2,1)}) fusion(), kind=kLoop, calls=%fused_computation.18 | loop fusion | flops 106954752 | bytes 25165824 | tf_op jit(solution)/shard_map/convert_element_type | solution.py:58
  162.4 104.7 %cosine_convert_fusion = (bf16[64,24,1,4096]{3,0,1,2:T(8,128)(2,1)}, bf16[64,24,1,4096]{3,0,1,2:T(8,128)(2,1)}) fusion(s32[64,24]{0,1:T(8,128)S(1)} %multiply_add_fusion), kind=kLoop, calls=%fused_computation.15 | loop fusion | flops 106954752 | bytes 25171968 | tf_op jit(solution)/shard_map/convert_element_type | solution.py:58
  267.1 6.4 %reshape.534 = bf16[3072,3,2,4]{3,2,1,0:T(2,128)(2,1)} reshape(bf16[64,2,576]{2,1,0:T(2,128)(2,1)S(1)} %all-to-all-done) | data formatting | bytes 294912
  273.5 11.2 %copy.243 = bf16[3,4,2,64,2,24]{5,4,3,2,1,0:T(2,128)(2,1)S(1)} copy(bf16[3,4,2,64,2,24]{1,2,0,5,4,3:T(2,128)(2,1)} %bitcast.121) | data formatting | bytes 294912 | tf_op jit(solution)/shard_map/reshape | solution.py:101
  284.7 0.7 broadcast_multiply_fusion
  285.4 0.7 copy.214
  286.1 10.3 %fusion.16 = f32[3,4,2,4096]{3,1,2,0:T(4,128)S(1)} fusion(bf16[3,4,2,64,2,24]{3,1,5,2,4,0:T(4,128)(2,1)S(1)} %copy.214, bf16[64,24,1,4096]{3,0,1,2:T(8,128)(2,1)} %get-tuple-element.29, bf16[64,24,1,4096]{3,0,1,2:T(8,128)(2,1)} %get-tuple-element.28), kind=kOutput, calls=%fused_computation.28 | convolution fusion | flops 616562688 | bytes 25706496 | tf_op jit(solution)/shard_map/qscbrn,bncj->qsrj/dot_general | solution.py:105
  296.5 11.8 %fusion.22 = bf16[2,4,2,1536,2]{3,1,4,0,2:T(4,128)(2,1)S(1)} fusion(bf16[1536,1,4096]{2,0,1:T(8,128)(2,1)} %get-tuple-element.36, bf16[1536,1,4096]{2,0,1:T(8,128)(2,1)} %get-tuple-element.37, bf16[1,4,2,4096]{3,1,2,0:T(4,128)(2,1)S(1)} %get-tuple-element.20, bf16[1,4,2,4096]{3,1,2,0:T(4,128)(2,1)S(1)} %get-tuple-element.19), kind=kOutput, calls=%fused_computation.34 | convolution fusion | flops 453345280 | bytes 25395200 | tf_op jit(solution)/shard_map/psrj,mcj->pscmr/dot_general | solution.py:110
  308.2 2.8 copy.215
  311.0 2.4 copy.216
  313.4 0.4 reshape.535
  313.8 8.3 %all_to_all.30 = bf16[4,2,6144]{2,1,0:T(2,128)(2,1)S(1)} all-to-all(bf16[4,2,6144]{2,1,0:T(2,128)(2,1)S(1)} %reshape.535), channel_id=1, replica_groups=mesh['sims'=4,'blk_0'=4,'blk_1'=4,'blk_2'=4] {'blk_0'}, dimensions={0} | all-to-all | bytes 196608 | tf_op jit(solution)/shard_map/all_to_all | solution.py:26
  322.1 0.2 reshape.536
  322.4 0.4 reshape.537
  322.8 8.8 %all_to_all.31 = bf16[4,2,6144]{2,1,0:T(2,128)(2,1)S(1)} all-to-all(bf16[4,2,6144]{2,1,0:T(2,128)(2,1)S(1)} %reshape.537), channel_id=1, replica_groups=mesh['sims'=4,'blk_0'=4,'blk_1'=4,'blk_2'=4] {'blk_1'}, dimensions={0} | all-to-all | bytes 196608 | tf_op jit(solution)/shard_map/all_to_all | solution.py:26
  331.7 0.2 reshape.538
  331.9 0.2 copy.269
  332.1 1.0 reshape.539
  333.1 4.0 all-to-all-start.3
  337.1 0.8 mul.379
  337.9 13.1 %copy.225 = bf16[24,1536,128]{1,0,2:T(8,128)(2,1)} copy(bf16[24,1536,128]{2,1,0:T(8,128)(2,1)} %param.10) | data formatting | bytes 18874368 | tf_op args[4]
  351.0 0.3 reshape.540
  351.3 0.3 copy.219
  352.1 14.7 %fusion.17 = f32[3,24,4,2,1536]{4,2,3,0,1:T(4,128)S(1)} fusion(bf16[24,1536,64,2,1,1]{1,0,3,2,5,4:T(8,128)(2,1)} %bitcast.119, bf16[1,4,2,64,24,2]{3,1,5,2,0,4:T(4,128)(2,1)S(1)} %copy.224, bf16[1,4,2,64,24,2]{3,1,5,2,0,4:T(4,128)(2,1)S(1)} %copy.221, bf16[1,4,2,64,24,2]{3,1,5,2,0,4:T(4,128)(2,1)S(1)} %multiply_convert_fusion.1), kind=kOutput, calls=%fused_computation.29 | convolution fusion | flops 226934784 | bytes 13123584 | tf_op jit(solution)/shard_map/kscbnr,nlbr->knscl/dot_general | solution.py:119
  366.8 0.8 slice_bitcast_fusion.2
  367.7 0.8 fusion.29
  368.5 1.0 fusion.26
  369.6 0.9 broadcast_in_dim.22
  370.4 10.1 %all-to-all-start.4 = ((bf16[4,24,2,1536]{3,1,2,0:T(8,128)(2,1)}), bf16[4,24,2,1536]{3,1,2,0:T(8,128)(2,1)S(1)}, u32[]{:S(2)}, u32[]{:S(2)}) async-start(bf16[4,24,2,1536]{3,1,2,0:T(8,128)(2,1)} %broadcast_in_dim.22), calls=%async_computation.4 | async-start | bytes 1179648 | tf_op jit(solution)/shard_map/all_to_all | solution.py:37
  380.6 0.5 stack.88
  381.0 0.5 stack.89
  381.5 13.2 %all-to-all-done.4 = bf16[4,24,2,1536]{3,1,2,0:T(8,128)(2,1)S(1)} async-done(((bf16[4,24,2,1536]{3,1,2,0:T(8,128)(2,1)}), bf16[4,24,2,1536]{3,1,2,0:T(8,128)(2,1)S(1)}, u32[]{:S(2)}, u32[]{:S(2)}) %all-to-all-start.4) | async-done | bytes 589856 | tf_op jit(solution)/shard_map/all_to_all | solution.py:37
  394.9 0.2 copy.230
  395.1 0.6 multiply_reduce_fusion.1
  395.7 0.2 fusion.35
  395.9 1.9 fusion.25
  397.9 7.0 %rev.3 = f32[24,2,2,2,1536]{4,2,1,0,3:T(2,128)S(1)} reverse(f32[24,2,2,2,1536]{4,2,1,0,3:T(2,128)} %fusion.25), dimensions={2} | reverse | bytes 2359296 | tf_op jit(solution)/shard_map/rev | solution.py:148
  404.9 1.4 multiply_reduce_fusion
  406.6 2.0 broadcast_in_dim.25
  408.6 11.7 %all-to-all-start.5 = ((bf16[64,4,2,1536]{3,2,1,0:T(2,128)(2,1)}), bf16[64,4,2,1536]{3,2,1,0:T(2,128)(2,1)S(1)}, u32[]{:S(2)}, u32[]{:S(2)}) async-start(bf16[64,4,2,1536]{3,2,1,0:T(2,128)(2,1)} %broadcast_in_dim.25), calls=%async_computation.5 | async-start | bytes 3145728 | tf_op jit(solution)/shard_map/all_to_all | solution.py:37
  420.3 0.7 copy.233
  421.0 38.5 %all-to-all-done.5 = bf16[64,4,2,1536]{3,2,1,0:T(2,128)(2,1)S(1)} async-done(((bf16[64,4,2,1536]{3,2,1,0:T(2,128)(2,1)}), bf16[64,4,2,1536]{3,2,1,0:T(2,128)(2,1)S(1)}, u32[]{:S(2)}, u32[]{:S(2)}) %all-to-all-start.5) | async-done | bytes 1572896 | tf_op jit(solution)/shard_map/all_to_all | solution.py:37
  459.5 0.5 convert_reduce_fusion
  460.0 0.6 broadcast_divide_fusion
  (60 shorter events, 2.7 us)
Async XLA Ops:
  0.7 23.9 %copy-start.3 = (f32[24]{0:T(128)}, f32[24]{0:T(128)S(1)}, u32[]{:S(2)}) copy-start(f32[24]{0:T(128)S(1)} %add_convert_fusion) | copy-start | bytes 292
  0.7 0.6 copy-start
  19.0 5.6 %copy-start.6 = (f32[128]{0:T(128)S(1)}, f32[128]{0:T(128)}, u32[]{:S(2)}) copy-start(f32[128]{0:T(128)} %param.9) | copy-start | bytes 1540
  24.7 0.5 copy-start.5
  48.6 218.5 %all-to-all-start = ((bf16[64,2,576]{2,1,0:T(2,128)(2,1)}), bf16[64,2,576]{2,1,0:T(2,128)(2,1)S(1)}, u32[]{:S(2)}, u32[]{:S(2)}) async-start(bf16[64,2,576]{2,1,0:T(2,128)(2,1)} %reshape.533), calls=%async_computation | async-start | bytes 327680 | tf_op jit(solution)/shard_map/all_to_all | solution.py:101
  162.4 104.7 %copy-start.2 = (s32[2,4096]{1,0:T(2,128)S(1)}, s32[2,4096]{1,0:T(2,128)}, u32[]{:S(2)}) copy-start(s32[2,4096]{1,0:T(2,128)} %param.11) | copy-start | bytes 98308
  333.1 17.9 %all-to-all-start.3 = ((bf16[4,2,6144]{2,1,0:T(2,128)(2,1)}), bf16[4,2,6144]{2,1,0:T(2,128)(2,1)S(1)}, u32[]{:S(2)}, u32[]{:S(2)}) async-start(bf16[4,2,6144]{2,1,0:T(2,128)(2,1)} %reshape.539), calls=%async_computation.3 | async-start | bytes 196608 | tf_op jit(solution)/shard_map/all_to_all | solution.py:26
  366.8 0.9 copy-start.4
  370.4 24.3 %all-to-all-start.4 = ((bf16[4,24,2,1536]{3,1,2,0:T(8,128)(2,1)}), bf16[4,24,2,1536]{3,1,2,0:T(8,128)(2,1)S(1)}, u32[]{:S(2)}, u32[]{:S(2)}) async-start(bf16[4,24,2,1536]{3,1,2,0:T(8,128)(2,1)} %broadcast_in_dim.22), calls=%async_computation.4 | async-start | bytes 1179648 | tf_op jit(solution)/shard_map/all_to_all | solution.py:37
  397.9 62.1 %copy-start.1 = (f32[1536]{0:T(1024)S(1)}, f32[1536]{0:T(1024)}, u32[]{:S(2)}) copy-start(f32[1536]{0:T(1024)} %copy-done) | copy-start | bytes 18436
  408.6 50.8 %all-to-all-start.5 = ((bf16[64,4,2,1536]{3,2,1,0:T(2,128)(2,1)}), bf16[64,4,2,1536]{3,2,1,0:T(2,128)(2,1)S(1)}, u32[]{:S(2)}, u32[]{:S(2)}) async-start(bf16[64,4,2,1536]{3,2,1,0:T(2,128)(2,1)} %broadcast_in_dim.25), calls=%async_computation.5 | async-start | bytes 3145728 | tf_op jit(solution)/shard_map/all_to_all | solution.py:37
where the time goes:
time: 465 us; the launch traced here: 461 us
  other arithmetic  223 us (48%)
  local copies, waits for them, and re-layouts  87.7 us (19%)
  waiting for transfers between devices  51.7 us (11%)
  matrix products  41.8 us (9%)
  starting transfers between devices  38.3 us (8%)
  blocking collectives  17.2 us (4%)
    convert_element_type x1, other arithmetic, fourier_table(): jnp.cos(phases).astype(jnp.bfloat16)  105 us
    convert_element_type x1, other arithmetic, fourier_table(): (-jnp.sin(phases)).astype(jnp.bfloat16)  101 us
    all_to_all x2, waiting for transfers between devices, from_everyone(): lax.all_to_all(jnp.broadcast_to(shard[None], (length, *shard.shape)), axi...  51.7 us
    unnamed x27, local copies, waits for them, and re-layouts  36.9 us
    all_to_all x2, starting transfers between devices, from_everyone(): lax.all_to_all(jnp.broadcast_to(shard[None], (length, *shard.shape)), axi...  21.8 us
    all_to_all x2, blocking collectives, exchange_in_order(): result = lax.all_to_all(result, axes[k], k, k, tiled=True)  17.2 us
    dot_general x1, matrix products, per_device(): jnp.einsum('kscbnr,nlbr->knscl', stacked, legendre_grid, preferred_elemen...  14.7 us
    all_to_all x1, starting transfers between devices, per_device(): lax.all_to_all(cycle_coefs, BLK, split_axis=3, concat_axis=3, tiled=True)  12.5 us
  transfers between devices with their start and end apart: 4, of which 2 were waited for; matrix products, arithmetic and copies ran while one was open for 48% of the time, Pallas kernels for 0%

commit v1 on v0

--- a/solution.py
+++ b/solution.py
@@ -98,9 +98,10 @@
     )
     pixel_weight = pixel_mask.astype(jnp.float32)
     legendre_grid = legendre.reshape(local_modes, degrees, blocks, cycle_local)
-    arranged = lax.all_to_all(cycle_coefs, BLK, split_axis=3, concat_axis=3, tiled=True).reshape(
-        3, -1, 2, blocks, cycle_local, local_modes
-    )
+    arranged = jnp.concatenate(
+        lax.all_to_all(jnp.stack(jnp.split(cycle_coefs, lax.axis_size(BLK), axis=3)), BLK, 0, 0),
+        axis=3,
+    ).reshape(3, -1, 2, blocks, cycle_local, local_modes)
     scaled = arranged * mode_weight
     cycle_maps = jnp.einsum(
         "qscbrn,bncj->qsrj", scaled, fourier_grid, preferred_element_type=jnp.float32

time: 465 us -> 433 us (0.931)
  local copies, waits for them, and re-layouts: 87.7 us -> 55.9 us
    unnamed x27 -> x90, local copies, waits for them, and re-layouts: 36.9 us -> 24.4 us
    reshape x1, local copies, waits for them, and re-layouts: 11.2 us -> 0.49 us  [per_device(): jnp.concatenate(lax.all_to_all(jnp.stack(jnp.split(cycle_coefs, lax.axis_...]
    another operation x2 -> x1, local copies, waits for them, and re-layouts: 8.4 us -> 0.34 us  [per_device(): jnp.stack([legsum[0], rotated, slopes], axis=0).astype(jnp.bfloat16)]
  transfers between devices with their start and end apart: 4 -> 4, of which waited for: 2 -> 2; matrix products, arithmetic and copies ran while one was open for 48% -> 52% of each run, Pallas kernels for 0% -> 0%
where the time goes in v1:
time: 433 us; the launch traced here: 429 us
  other arithmetic  222 us (51%)
  local copies, waits for them, and re-layouts  55.9 us (13%)
  waiting for transfers between devices  51.7 us (12%)
  matrix products  41.9 us (10%)
  starting transfers between devices  38.5 us (9%)
  blocking collectives  17.3 us (4%)
    convert_element_type x1, other arithmetic, fourier_table(): jnp.cos(phases).astype(jnp.bfloat16)  105 us
    convert_element_type x1, other arithmetic, fourier_table(): (-jnp.sin(phases)).astype(jnp.bfloat16)  101 us
    all_to_all x2, waiting for transfers between devices, from_everyone(): lax.all_to_all(jnp.broadcast_to(shard[None], (length, *shard.shape)), axi...  51.7 us
    unnamed x90, local copies, waits for them, and re-layouts  24.4 us
    all_to_all x2, starting transfers between devices, from_everyone(): lax.all_to_all(jnp.broadcast_to(shard[None], (length, *shard.shape)), axi...  21.8 us
    all_to_all x2, blocking collectives, exchange_in_order(): result = lax.all_to_all(result, axes[k], k, k, tiled=True)  17.3 us
    dot_general x1, matrix products, per_device(): jnp.einsum('kscbnr,nlbr->knscl', stacked, legendre_grid, preferred_elemen...  14.7 us
    all_to_all x1, starting transfers between devices, per_device(): lax.all_to_all(jnp.stack(jnp.split(cycle_coefs, lax.axis_size(BLK), axis=...  12.8 us
  transfers between devices with their start and end apart: 4, of which 2 were waited for; matrix products, arithmetic and copies ran while one was open for 52% of the time, Pallas kernels for 0%

profile of v1, /device:TPU:1, one launch (start us, length us, event | category | flops | bytes accessed | tf_op | source)
XLA Modules:
  0.0 428.8 jit_solution(13947730931923651965)
XLA Ops:
  0.7 0.1 sqrt_select_fusion
  0.9 0.5 copy-done
  1.4 2.4 convert_bitcast_fusion
  3.8 1.3 fusion.24
  5.1 0.5 pad_bitcast_fusion
  5.6 4.6 %pad_maximum_fusion = bf16[24,4,4,2,1536]{4,3,2,0,1:T(2,128)(2,1)S(1)} fusion(bf16[24,1,4,2,1536]{4,3,2,0,1:T(2,128)(2,1)S(1)} %pad_bitcast_fusion, bf16[24,1,4,2,1536]{4,3,2,0,1:T(2,128)(2,1)S(1)} %get-tuple-element.16, bf16[24,1,4,2,1536]{4,3,2,0,1:T(2,128)(2,1)S(1)} %get-tuple-element.15, bf16[24,1,4,2,1536]{4,3,2,0,1:T(2,128)(2,1)S(1)} %get-tuple-element.18), kind=kLoop, calls=%fused_computation.31 | loop fusion | flops 3538944 | bytes 4718592 | tf_op jit(solution)/shard_map/stack | solution.py:82
  10.2 3.9 copy.174
  14.0 5.0 %convert_element_type.158 = bf16[24,32,1536]{2,1,0:T(8,128)(2,1)S(1)} reshape(bf16[24,4,4,2,1536]{4,3,2,1,0:T(2,128)(2,1)} %copy.174) | data formatting | bytes 4718592 | tf_op jit(solution)/shard_map/convert_element_type | solution.py:82
  19.0 4.6 %convolution_bitcast_fusion = f32[32,128,24]{1,0,2:T(8,128)S(1)} fusion(bf16[24,32,1536]{2,1,0:T(8,128)(2,1)S(1)} %convert_element_type.158, bf16[24,1536,128]{2,1,0:T(8,128)(2,1)} %param.10), kind=kOutput, calls=%fused_computation.37 | convolution fusion | flops 301989888 | bytes 12189696 | tf_op jit(solution)/shard_map/mkl,mlr->krm/dot_general | solution.py:86
  24.0 0.2 stack.353
  24.3 0.2 stack.354
  24.7 0.5 copy-done.5
  25.4 0.2 copy.180
  25.6 0.3 squeeze.15
  26.0 0.2 copy.181
  26.2 0.3 squeeze.16
  26.7 0.2 copy.175
  26.9 0.3 stack.273
  27.4 0.2 pad_maximum_fusion.1
  32.6 1.3 reshape.533
  33.9 12.8 %all-to-all-start = ((bf16[64,2,576]{2,1,0:T(2,128)(2,1)}), bf16[64,2,576]{2,1,0:T(2,128)(2,1)S(1)}, u32[]{:S(2)}, u32[]{:S(2)}) async-start(bf16[64,2,576]{2,1,0:T(2,128)(2,1)} %reshape.533), calls=%async_computation | async-start | bytes 327680 | tf_op jit(solution)/shard_map/all_to_all | solution.py:102
  46.6 101.2 %negate_convert_fusion.1 = (bf16[1536,1,4096]{2,0,1:T(8,128)(2,1)}, bf16[1536,1,4096]{2,0,1:T(8,128)(2,1)}) fusion(), kind=kLoop, calls=%fused_computation.18 | loop fusion | flops 106954752 | bytes 25165824 | tf_op jit(solution)/shard_map/convert_element_type | solution.py:58
  147.9 104.7 %cosine_convert_fusion = (bf16[64,24,1,4096]{3,0,1,2:T(8,128)(2,1)}, bf16[64,24,1,4096]{3,0,1,2:T(8,128)(2,1)}) fusion(s32[64,24]{0,1:T(8,128)S(1)} %multiply_add_fusion), kind=kLoop, calls=%fused_computation.15 | loop fusion | flops 106954752 | bytes 25171968 | tf_op jit(solution)/shard_map/convert_element_type | solution.py:58
  252.6 0.5 reshape.534
  253.1 0.5 copy.182
  253.6 10.4 %fusion.16 = f32[3,4,2,4096]{3,1,2,0:T(4,128)S(1)} fusion(bf16[64,24,1,4096]{3,0,1,2:T(8,128)(2,1)} %get-tuple-element.29, bf16[64,24,1,4096]{3,0,1,2:T(8,128)(2,1)} %get-tuple-element.28, bf16[3,4,2,64,2,24]{3,5,4,2,1,0:T(8,128)(2,1)S(1)} %broadcast_multiply_fusion.1), kind=kOutput, calls=%fused_computation.28 | convolution fusion | flops 616562688 | bytes 25706496 | tf_op jit(solution)/shard_map/qscbrn,bncj->qsrj/dot_general | solution.py:106
  264.1 11.8 %fusion.22 = bf16[2,4,2,1536,2]{3,1,4,0,2:T(4,128)(2,1)S(1)} fusion(bf16[1536,1,4096]{2,0,1:T(8,128)(2,1)} %get-tuple-element.36, bf16[1536,1,4096]{2,0,1:T(8,128)(2,1)} %get-tuple-element.37, bf16[1,4,2,4096]{3,1,2,0:T(4,128)(2,1)S(1)} %get-tuple-element.20, bf16[1,4,2,4096]{3,1,2,0:T(4,128)(2,1)S(1)} %get-tuple-element.19), kind=kOutput, calls=%fused_computation.34 | convolution fusion | flops 453345280 | bytes 25395200 | tf_op jit(solution)/shard_map/psrj,mcj->pscmr/dot_general | solution.py:111
  275.9 2.8 copy.184
  278.6 2.4 copy.185
  281.0 0.4 reshape.535
  281.4 8.4 %all_to_all.30 = bf16[4,2,6144]{2,1,0:T(2,128)(2,1)S(1)} all-to-all(bf16[4,2,6144]{2,1,0:T(2,128)(2,1)S(1)} %reshape.535), channel_id=1, replica_groups=mesh['sims'=4,'blk_0'=4,'blk_1'=4,'blk_2'=4] {'blk_0'}, dimensions={0} | all-to-all | bytes 196608 | tf_op jit(solution)/shard_map/all_to_all | solution.py:26
  289.9 0.2 reshape.536
  290.2 0.4 reshape.537
  290.6 8.8 %all_to_all.31 = bf16[4,2,6144]{2,1,0:T(2,128)(2,1)S(1)} all-to-all(bf16[4,2,6144]{2,1,0:T(2,128)(2,1)S(1)} %reshape.537), channel_id=1, replica_groups=mesh['sims'=4,'blk_0'=4,'blk_1'=4,'blk_2'=4] {'blk_1'}, dimensions={0} | all-to-all | bytes 196608 | tf_op jit(solution)/shard_map/all_to_all | solution.py:26
  299.4 0.2 reshape.538
  299.7 0.2 copy.239
  299.9 1.0 reshape.539
  300.9 4.0 all-to-all-start.3
  304.9 0.8 mul.379
  305.7 13.3 %copy.194 = bf16[24,1536,128]{1,0,2:T(8,128)(2,1)} copy(bf16[24,1536,128]{2,1,0:T(8,128)(2,1)} %param.10) | data formatting | bytes 18874368 | tf_op args[4]
  319.0 0.3 reshape.540
  319.3 0.3 copy.188
  320.1 14.7 %fusion.17 = f32[3,24,4,2,1536]{4,2,3,0,1:T(4,128)S(1)} fusion(bf16[24,1536,64,2,1,1]{1,0,3,2,5,4:T(8,128)(2,1)} %bitcast.373, bf16[1,4,2,64,24,2]{3,1,5,2,0,4:T(4,128)(2,1)S(1)} %copy.193, bf16[1,4,2,64,24,2]{3,1,5,2,0,4:T(4,128)(2,1)S(1)} %copy.190, bf16[1,4,2,64,24,2]{3,1,5,2,0,4:T(4,128)(2,1)S(1)} %multiply_convert_fusion.1), kind=kOutput, calls=%fused_computation.29 | convolution fusion | flops 226934784 | bytes 13123584 | tf_op jit(solution)/shard_map/kscbnr,nlbr->knscl/dot_general | solution.py:120
  334.8 0.8 slice_bitcast_fusion.2
  335.6 0.8 fusion.29
  336.5 1.0 fusion.26
  337.5 0.9 broadcast_in_dim.22
  338.4 10.1 %all-to-all-start.4 = ((bf16[4,24,2,1536]{3,1,2,0:T(8,128)(2,1)}), bf16[4,24,2,1536]{3,1,2,0:T(8,128)(2,1)S(1)}, u32[]{:S(2)}, u32[]{:S(2)}) async-start(bf16[4,24,2,1536]{3,1,2,0:T(8,128)(2,1)} %broadcast_in_dim.22), calls=%async_computation.4 | async-start | bytes 1179648 | tf_op jit(solution)/shard_map/all_to_all | solution.py:37
  348.5 0.5 stack.348
  349.0 0.5 stack.349
  349.5 13.2 %all-to-all-done.4 = bf16[4,24,2,1536]{3,1,2,0:T(8,128)(2,1)S(1)} async-done(((bf16[4,24,2,1536]{3,1,2,0:T(8,128)(2,1)}), bf16[4,24,2,1536]{3,1,2,0:T(8,128)(2,1)S(1)}, u32[]{:S(2)}, u32[]{:S(2)}) %all-to-all-start.4) | async-done | bytes 589856 | tf_op jit(solution)/shard_map/all_to_all | solution.py:37
  362.8 0.2 copy.199
  363.1 0.6 multiply_reduce_fusion.1
  363.7 0.2 fusion.35
  363.9 1.9 fusion.25
  365.8 7.0 %rev.3 = f32[24,2,2,2,1536]{4,2,1,0,3:T(2,128)S(1)} reverse(f32[24,2,2,2,1536]{4,2,1,0,3:T(2,128)} %fusion.25), dimensions={2} | reverse | bytes 2359296 | tf_op jit(solution)/shard_map/rev | solution.py:149
  372.9 1.4 multiply_reduce_fusion
  374.3 0.2 fusion.52
  374.6 2.0 broadcast_in_dim.25
  376.6 11.7 %all-to-all-start.5 = ((bf16[64,4,2,1536]{3,2,1,0:T(2,128)(2,1)}), bf16[64,4,2,1536]{3,2,1,0:T(2,128)(2,1)S(1)}, u32[]{:S(2)}, u32[]{:S(2)}) async-start(bf16[64,4,2,1536]{3,2,1,0:T(2,128)(2,1)} %broadcast_in_dim.25), calls=%async_computation.5 | async-start | bytes 3145728 | tf_op jit(solution)/shard_map/all_to_all | solution.py:37
  388.3 0.7 copy.202
  388.9 38.5 %all-to-all-done.5 = bf16[64,4,2,1536]{3,2,1,0:T(2,128)(2,1)S(1)} async-done(((bf16[64,4,2,1536]{3,2,1,0:T(2,128)(2,1)}), bf16[64,4,2,1536]{3,2,1,0:T(2,128)(2,1)S(1)}, u32[]{:S(2)}, u32[]{:S(2)}) %all-to-all-start.5) | async-done | bytes 1572896 | tf_op jit(solution)/shard_map/all_to_all | solution.py:37
  427.4 0.5 convert_reduce_fusion
  428.0 0.6 broadcast_divide_fusion
  (122 shorter events, 7.0 us)
Async XLA Ops:
  0.7 23.9 %copy-start.3 = (f32[24]{0:T(128)}, f32[24]{0:T(128)S(1)}, u32[]{:S(2)}) copy-start(f32[24]{0:T(128)S(1)} %add_convert_fusion) | copy-start | bytes 292
  0.7 0.6 copy-start
  19.0 5.6 %copy-start.6 = (f32[128]{0:T(128)S(1)}, f32[128]{0:T(128)}, u32[]{:S(2)}) copy-start(f32[128]{0:T(128)} %param.9) | copy-start | bytes 1540
  24.7 0.5 copy-start.5
  33.9 218.7 %all-to-all-start = ((bf16[64,2,576]{2,1,0:T(2,128)(2,1)}), bf16[64,2,576]{2,1,0:T(2,128)(2,1)S(1)}, u32[]{:S(2)}, u32[]{:S(2)}) async-start(bf16[64,2,576]{2,1,0:T(2,128)(2,1)} %reshape.533), calls=%async_computation | async-start | bytes 327680 | tf_op jit(solution)/shard_map/all_to_all | solution.py:102
  147.9 104.7 %copy-start.2 = (s32[2,4096]{1,0:T(2,128)S(1)}, s32[2,4096]{1,0:T(2,128)}, u32[]{:S(2)}) copy-start(s32[2,4096]{1,0:T(2,128)} %param.11) | copy-start | bytes 98308
  300.9 18.1 %all-to-all-start.3 = ((bf16[4,2,6144]{2,1,0:T(2,128)(2,1)}), bf16[4,2,6144]{2,1,0:T(2,128)(2,1)S(1)}, u32[]{:S(2)}, u32[]{:S(2)}) async-start(bf16[4,2,6144]{2,1,0:T(2,128)(2,1)} %reshape.539), calls=%async_computation.3 | async-start | bytes 196608 | tf_op jit(solution)/shard_map/all_to_all | solution.py:26
  334.8 0.9 copy-start.4
  338.4 24.3 %all-to-all-start.4 = ((bf16[4,24,2,1536]{3,1,2,0:T(8,128)(2,1)}), bf16[4,24,2,1536]{3,1,2,0:T(8,128)(2,1)S(1)}, u32[]{:S(2)}, u32[]{:S(2)}) async-start(bf16[4,24,2,1536]{3,1,2,0:T(8,128)(2,1)} %broadcast_in_dim.22), calls=%async_computation.4 | async-start | bytes 1179648 | tf_op jit(solution)/shard_map/all_to_all | solution.py:37
  365.8 62.1 %copy-start.1 = (f32[1536]{0:T(1024)S(1)}, f32[1536]{0:T(1024)}, u32[]{:S(2)}) copy-start(f32[1536]{0:T(1024)} %copy-done) | copy-start | bytes 18436
  376.6 50.8 %all-to-all-start.5 = ((bf16[64,4,2,1536]{3,2,1,0:T(2,128)(2,1)}), bf16[64,4,2,1536]{3,2,1,0:T(2,128)(2,1)S(1)}, u32[]{:S(2)}, u32[]{:S(2)}) async-start(bf16[64,4,2,1536]{3,2,1,0:T(2,128)(2,1)} %broadcast_in_dim.25), calls=%async_computation.5 | async-start | bytes 3145728 | tf_op jit(solution)/shard_map/all_to_all | solution.py:37
